TPU v7x, 256 devices: a whole 4x4x8 slice. The times are simulated.
256 devices in a mesh: client: 16 (over y_lo, z), tensor: 8 (over x, core), sdata: 2 (over y_hi).
Axes of the slice: x: 4, y: 4 (y_hi: 2, y_lo: 2; y = y_hi * 2 + y_lo), z: 8, core: 2. Of those that a mesh axis runs over, the one named last changes fastest.
Arguments:
- client_input: bfloat16 [12288, 2048], P(('client', 'sdata')), may hold values from -6 to 6
- client_gain: bfloat16 [16, 2048], P('client'), may hold values from 0.5 to 1.5
- query_weight: bfloat16 [16, 2048, 2048], P('client', None, 'tensor'), as said below
- key_weight: bfloat16 [16, 2048, 512], P('client', None, 'tensor'), as said below
- client_value_weight: bfloat16 [16, 2048, 512], P('client', None, 'tensor'), may hold values from -0.125 to 0.125
- output_weight: bfloat16 [16, 2048, 2048], P('client', None, 'tensor'), may hold values from -0.125 to 0.125
- server_gain: bfloat16 [2, 2048], P('sdata'), may hold values from 0.5 to 1.5
- server_gate: bfloat16 [2, 2048, 4096], P('sdata', None, 'tensor'), may hold values from -0.125 to 0.125
- server_up: bfloat16 [2, 2048, 4096], P('sdata', None, 'tensor'), may hold values from -0.125 to 0.125
- server_down: bfloat16 [2, 4096, 2048], P('sdata', 'tensor'), may hold values from -0.09375 to 0.09375
- upstream: bfloat16 [12288, 2048], P(('client', 'sdata')), may hold values from -6 to 6
- assignment: int32 [16], replicated, may hold values from 0 to 1, as said below
Outputs:
- query_update: bfloat16 [2048, 2048], P(('client', 'sdata'), 'tensor')
- key_update: bfloat16 [2048, 512], P(('client', 'sdata'), 'tensor')
- value_update: bfloat16 [2048, 512], P(('client', 'sdata'), 'tensor')
- output_update: bfloat16 [2048, 2048], P(('client', 'sdata'), 'tensor')
Inputs may be any that keep to these rules, and one draw needn't show every extreme that they name: `assignment`: each of the 2 server groups is named by exactly 8 clients. `query_weight`: independent entries with a spread of about 2048 ** -0.5. `key_weight`: entries with a spread of about 2048 ** -0.5 or more.
All inputs are finite; a program needn't handle non-finite values.
Results may differ from a plain program's by a relative error of at most 0.038.
The roundings to bfloat16 on the way count: a program that leaves them out, or rounds other values in their place, can miss the bound.
Values may be sent and summed in bfloat16 or wider, within the bound.
No kernel may reach another device: no remote copies, remote signals or barrier semaphores. Data moves between devices by JAX's collectives and lax.ppermute only.
A program may use at most 128 MiB of HBM per device.

v0:
```python
from functools import partial
import math
import jax
import jax.numpy as jnp
from jax import lax
from jax.sharding import PartitionSpec as P

HEAD_DIM = 64


def cut_along(value, dim, length):
    before, after = (value.shape[:dim], value.shape[dim + 1 :])
    return jnp.moveaxis(value.reshape(*before, length, -1, *after), dim, 0)


def sum_at_owner(value, axis, dim):
    length = lax.axis_size(axis)
    tiles = lax.all_to_all(cut_along(value, dim, length), axis, 0, 0, tiled=True)
    return jnp.sum(tiles.astype(jnp.float32), axis=0)


def rotary_tables(length):
    halfway = HEAD_DIM // 2
    positions = jnp.arange(length).astype(jnp.float32)
    exponents = jnp.arange(halfway).astype(jnp.float32) * (2.0 / HEAD_DIM)
    frequencies = jnp.exp(-math.log(500000.0) * exponents)
    angles = positions[:, None] * frequencies[None, :]
    cosine_table = jnp.concatenate([jnp.cos(angles), jnp.cos(angles)], 1)
    sine_table = jnp.concatenate([jnp.sin(angles), jnp.sin(angles)], 1)
    return (cosine_table, sine_table)


def rotary(heads_in, cosine_table, sine_table):
    halfway = heads_in.shape[-1] // 2
    turned = jnp.concatenate([-heads_in[..., halfway:], heads_in[..., :halfway]], -1)
    return heads_in * cosine_table[:, None, :] + turned * sine_table[:, None, :]


def normalize(rows_in, gain):
    rows_float = rows_in.astype(jnp.float32)
    inv_rms = lax.rsqrt(jnp.mean(rows_float * rows_float, -1, keepdims=True) + 1e-05)
    return (rows_float * inv_rms * gain.astype(jnp.float32)).astype(jnp.bfloat16)


def attention_part(normed, query_matrix, client_key_matrix, value_matrix, output_matrix):
    length = normed.shape[0]
    query_count = query_matrix.shape[1] // HEAD_DIM
    shared_count = client_key_matrix.shape[1] // HEAD_DIM
    group_size = query_count // shared_count
    cosine_table, sine_table = rotary_tables(length)
    queries = jnp.dot(normed, query_matrix, preferred_element_type=jnp.float32).reshape(
        length, query_count, HEAD_DIM
    )
    queries = (
        rotary(queries, cosine_table, sine_table)
        .astype(jnp.bfloat16)
        .reshape(length, shared_count, group_size, HEAD_DIM)
    )
    key_heads = jnp.dot(normed, client_key_matrix, preferred_element_type=jnp.float32).reshape(
        length, shared_count, HEAD_DIM
    )
    key_heads = rotary(key_heads, cosine_table, sine_table).astype(jnp.bfloat16)
    value_heads = (
        jnp.dot(normed, value_matrix, preferred_element_type=jnp.float32)
        .astype(jnp.bfloat16)
        .reshape(length, shared_count, HEAD_DIM)
    )
    scores = jnp.einsum(
        "qgrd,kgd->grqk", queries.astype(jnp.float32), key_heads.astype(jnp.float32)
    ) * HEAD_DIM ** (-0.5)
    row_ids = lax.broadcasted_iota(jnp.int32, (length, length), 0)
    col_ids = lax.broadcasted_iota(jnp.int32, (length, length), 1)
    scores = jnp.where(col_ids <= row_ids, scores, -1e30)
    highest = lax.stop_gradient(jnp.max(scores, -1, keepdims=True))
    exponent = jnp.exp(scores - highest)
    weights = (exponent / jnp.sum(exponent, -1, keepdims=True)).astype(jnp.bfloat16)
    context = jnp.einsum(
        "grqk,kgd->qgrd", weights.astype(jnp.float32), value_heads.astype(jnp.float32)
    )
    context = context.astype(jnp.bfloat16).reshape(length, query_count * HEAD_DIM)
    return lax.dot_general(
        context, output_matrix, (((1,), (1,)), ((), ())), preferred_element_type=jnp.float32
    )


def server_pull(rows_in, upstream_rows, gain, gate_matrix, up_matrix, down_matrix):
    rows_float = rows_in.astype(jnp.float32)
    inv_rms = lax.rsqrt(jnp.mean(rows_float * rows_float, -1, keepdims=True) + 1e-05)
    gain_float = gain.astype(jnp.float32)
    server_normed = (rows_float * inv_rms * gain_float).astype(jnp.bfloat16)
    gate_value = jnp.dot(server_normed, gate_matrix, preferred_element_type=jnp.float32)
    up_value = jnp.dot(server_normed, up_matrix, preferred_element_type=jnp.float32)
    pulled = lax.dot_general(
        upstream_rows, down_matrix, (((1,), (1,)), ((), ())), preferred_element_type=jnp.float32
    )
    sigmoid_gate = jax.nn.sigmoid(gate_value)
    gate_grad = (
        pulled * up_value * sigmoid_gate * (1.0 + gate_value * (1.0 - sigmoid_gate))
    ).astype(jnp.bfloat16)
    up_grad = (pulled * gate_value * sigmoid_gate).astype(jnp.bfloat16)
    normed_grad = lax.dot_general(
        gate_grad, gate_matrix, (((1,), (1,)), ((), ())), preferred_element_type=jnp.float32
    )
    normed_grad = normed_grad + lax.dot_general(
        up_grad, up_matrix, (((1,), (1,)), ((), ())), preferred_element_type=jnp.float32
    )
    weighted = normed_grad * gain_float
    return inv_rms * weighted - rows_float * inv_rms**3 * jnp.mean(
        weighted * rows_float, -1, keepdims=True
    )


def over_clients(pieces):
    return lax.all_to_all(pieces, "client", split_axis=1, concat_axis=1, tiled=True)


def over_groups(pieces):
    return lax.all_to_all(pieces, "sdata", split_axis=1, concat_axis=1, tiled=True)


def relay_out(stacked, group_order, client_count):
    count_rows, length, breadth = stacked.shape
    pieces = stacked.reshape(count_rows, client_count, length // client_count, breadth)
    arrived = jnp.take(over_clients(pieces), group_order, axis=1)
    return over_groups(arrived).reshape(count_rows, length, breadth)


def relay_back(stacked, inverse, client_count):
    count_rows, length, breadth = stacked.shape
    pieces = stacked.reshape(count_rows, client_count, length // client_count, breadth)
    arrived = jnp.take(over_groups(pieces), inverse, axis=1)
    return over_clients(arrived).reshape(count_rows, length, breadth)


def share_sum(partial_rows):
    return sum_at_owner(partial_rows.astype(jnp.bfloat16), "tensor", 1)


def widen_rows(stacked):
    return lax.all_gather(stacked, "tensor", axis=2, tiled=True)


def local(
    client_input,
    client_gain,
    query_weight,
    key_weight,
    client_value_weight,
    output_weight,
    server_gain,
    server_gate,
    server_up,
    server_down,
    upstream,
    assignment,
):
    client_count = lax.axis_size("client")
    normed = normalize(client_input, client_gain[0])
    attended, pullback = jax.vjp(
        partial(attention_part, normed),
        query_weight[0],
        key_weight[0],
        client_value_weight[0],
        output_weight[0],
    )
    group_order = jnp.argsort(assignment, stable=True)
    inverse = jnp.argsort(group_order, stable=True)
    shard_width = client_input.shape[1] // lax.axis_size("tensor")
    shard_start = lax.axis_index("tensor") * shard_width
    own_input = lax.dynamic_slice_in_dim(client_input, shard_start, shard_width, 1)
    own_upstream = lax.dynamic_slice_in_dim(upstream, shard_start, shard_width, 1)
    cut_input = (own_input.astype(jnp.float32) + share_sum(attended)).astype(jnp.bfloat16)
    arrived = relay_out(jnp.stack([cut_input, own_upstream]), group_order, client_count)
    widened = widen_rows(arrived)
    pulled = server_pull(
        widened[0], widened[1], server_gain[0], server_gate[0], server_up[0], server_down[0]
    )
    cut_grad = (share_sum(pulled) + arrived[1].astype(jnp.float32)).astype(jnp.bfloat16)
    returned = relay_back(cut_grad[None], inverse, client_count)
    arriving_grad = widen_rows(returned)[0]
    query_grad, key_grad, value_grad, output_grad = pullback(arriving_grad.astype(jnp.float32))
    query_width = query_grad.shape[1]
    key_width = key_grad.shape[1]
    joined_grads = jnp.concatenate(
        [
            query_grad.astype(jnp.float32),
            key_grad.astype(jnp.float32),
            value_grad.astype(jnp.float32),
            output_grad.astype(jnp.float32),
        ],
        1,
    )
    summed = sum_at_owner(joined_grads.astype(jnp.bfloat16), ("client", "sdata"), 0) / client_count
    query_update = summed[:, :query_width].astype(jnp.bfloat16)
    key_update = summed[:, query_width : query_width + key_width].astype(jnp.bfloat16)
    value_update = summed[:, query_width + key_width : query_width + 2 * key_width].astype(
        jnp.bfloat16
    )
    output_update = summed[:, query_width + 2 * key_width :].astype(jnp.bfloat16)
    return (query_update, key_update, value_update, output_update)


def solution(mesh):
    placed = (
        P(("client", "sdata"), None),
        P("client", None),
        P("client", None, "tensor"),
        P("client", None, "tensor"),
        P("client", None, "tensor"),
        P("client", None, "tensor"),
        P("sdata", None),
        P("sdata", None, "tensor"),
        P("sdata", None, "tensor"),
        P("sdata", "tensor", None),
        P(("client", "sdata"), None),
        P(),
    )
    return jax.shard_map(
        local,
        mesh=mesh,
        in_specs=placed,
        out_specs=(
            P(("client", "sdata"), "tensor"),
            P(("client", "sdata"), "tensor"),
            P(("client", "sdata"), "tensor"),
            P(("client", "sdata"), "tensor"),
        ),
        check_vma=False,
    )
```

profile of v0, /device:TPU:4, one launch (start us, length us, event | category | flops | bytes accessed | tf_op | source)
XLA Modules:
  0.0 317.1 jit_solution(7294213297382398546)
XLA Ops:
  8.1 1.9 fusion.3
  10.0 2.1 fusion.91
  12.2 1.4 copy.27
  13.6 2.6 fusion.36
  23.1 6.4 %all-to-all-start = ((bf16[8,384,256]{2,1,0:T(8,128)(2,1)}), bf16[8,384,256]{2,1,0:T(8,128)(2,1)}, u32[]{:S(2)}, u32[]{:S(2)}) async-start(bf16[8,384,256]{2,1,0:T(8,128)(2,1)} %bitcast.249), calls=%async_computation | async-start | bytes 3145728 | tf_op jit(solution)/shard_map/all_to_all | solution.py:18
  30.5 17.5 %all-to-all-done = bf16[8,384,256]{2,1,0:T(8,128)(2,1)} async-done(((bf16[8,384,256]{2,1,0:T(8,128)(2,1)}), bf16[8,384,256]{2,1,0:T(8,128)(2,1)}, u32[]{:S(2)}, u32[]{:S(2)}) %all-to-all-start) | async-done | bytes 1572896 | tf_op jit(solution)/shard_map/all_to_all | solution.py:18
  48.1 1.7 convert_reduce_fusion.2
  51.5 8.0 %all-to-all-start.1 = ((bf16[2,16,24,256]{3,2,0,1:T(8,128)(2,1)}), bf16[2,16,24,256]{3,2,0,1:T(8,128)(2,1)S(1)}, u32[]{:S(2)}, u32[]{:S(2)}) async-start(bf16[2,16,24,256]{3,2,0,1:T(8,128)(2,1)} %pad_maximum_fusion.1), calls=%async_computation.1 | async-start | bytes 786432 | tf_op jit(solution)/shard_map/all_to_all | solution.py:114
  59.6 1.3 sort.31
  62.1 10.1 %all-to-all-done.1 = bf16[2,16,24,256]{3,2,0,1:T(8,128)(2,1)S(1)} async-done(((bf16[2,16,24,256]{3,2,0,1:T(8,128)(2,1)}), bf16[2,16,24,256]{3,2,0,1:T(8,128)(2,1)S(1)}, u32[]{:S(2)}, u32[]{:S(2)}) %all-to-all-start.1) | async-done | bytes 393248 | tf_op jit(solution)/shard_map/all_to_all | solution.py:114
  73.0 1.6 gather_fusion
  74.6 11.3 %all_to_all.35 = bf16[2,16,24,256]{3,2,0,1:T(8,128)(2,1)S(1)} all-to-all(bf16[2,16,24,256]{3,2,0,1:T(8,128)(2,1)S(1)} %select_bitcast_fusion), channel_id=1, replica_groups=mesh['client'=16,'tensor'=8,'sdata'=2] {'sdata'}, dimensions={1} | all-to-all | bytes 786432 | tf_op jit(solution)/shard_map/all_to_all | solution.py:118
  87.5 29.4 %all-gather.3.cloned.1.call-done = bf16[2,384,2048]{2,1,0:T(8,128)(2,1)} async-done(((bf16[2,384,256]{2,1,0:T(8,128)(2,1)}), bf16[2,384,2048]{2,1,0:T(8,128)(2,1)}) %all-gather.3.cloned.1.call-update) | async-done | bytes 3145744 | tf_op jit(solution)/shard_map/all_gather | solution.py:140
  116.9 1.8 fusion.6
  119.3 4.1 %fusion.29 = f32[384,512]{1,0:T(8,128)} fusion(bf16[1,512,2048]{2,1,0:T(8,128)(2,1)} %param.21, bf16[2,384,2048]{2,1,0:T(8,128)(2,1)} %all-gather.3.cloned.1.call-done), kind=kOutput, calls=%fused_computation.50 | convolution fusion | flops 805306368 | bytes 4456448 | tf_op jit(solution)/shard_map/dot_general | solution.py:93
  123.5 1.9 fusion.24
  125.4 6.3 %fusion.22 = f32[384,2048]{1,0:T(8,128)} fusion(bf16[1,2048,512]{2,1,0:T(8,128)(2,1)} %param.19, f32[384,512]{1,0:T(8,128)} %fusion.29, bf16[1,2048,512]{2,1,0:T(8,128)(2,1)S(1)} %copy-done, f32[384,512]{1,0:T(8,128)} %fusion.24, f32[2048]{0:T(1024)S(1)} %bitcast.271, f32[384]{0:T(512)} %copy-done.29, bf16[2,384,2048]{2,1,0:T(8,128)(2,1)} %all-gather.3.cloned.1.call-done), kind=kOutput, calls=%fused_computation.43 | convolution fusion | flops 1615724544 | bytes 10496000 | tf_op jit(solution)/shard_map/dot_general | solution.py:101
  131.7 4.2 %fusion.10 = (f32[384]{0:T(512)S(1)}, f32[384,2048]{1,0:T(8,128)S(1)}) fusion(bf16[2,384,2048]{2,1,0:T(8,128)(2,1)} %all-gather.3.cloned.1.call-done, f32[2048]{0:T(1024)S(1)} %bitcast.272, f32[384,2048]{1,0:T(8,128)} %fusion.22, bf16[1,2048,512]{2,1,0:T(8,128)(2,1)S(1)} %copy-done, f32[384,512]{1,0:T(8,128)} %fusion.29, f32[384,512]{1,0:T(8,128)} %fusion.24), kind=kOutput, calls=%fused_computation.17 | convolution fusion | flops 810417792 | bytes 11544064 | tf_op jit(solution)/shard_map/dot_general | solution.py:104
  137.8 5.0 %all-to-all-start.3 = ((bf16[8,384,256]{2,1,0:T(8,128)(2,1)}), bf16[8,384,256]{2,1,0:T(8,128)(2,1)}, u32[]{:S(2)}, u32[]{:S(2)}) async-start(bf16[8,384,256]{2,1,0:T(8,128)(2,1)} %bitcast.250), calls=%async_computation.3 | async-start | bytes 3145728 | tf_op jit(solution)/shard_map/all_to_all | solution.py:18
  143.3 1.9 sort.32
  147.5 13.8 %all-to-all-done.3 = bf16[8,384,256]{2,1,0:T(8,128)(2,1)} async-done(((bf16[8,384,256]{2,1,0:T(8,128)(2,1)}), bf16[8,384,256]{2,1,0:T(8,128)(2,1)}, u32[]{:S(2)}, u32[]{:S(2)}) %all-to-all-start.3) | async-done | bytes 1572896 | tf_op jit(solution)/shard_map/all_to_all | solution.py:18
  161.3 1.7 convert_reduce_fusion.1
  163.7 4.4 %all-to-all-start.4 = ((bf16[1,16,24,256]{3,2,0,1:T(8,128)(2,1)}), bf16[1,16,24,256]{3,2,0,1:T(8,128)(2,1)S(1)}, u32[]{:S(2)}, u32[]{:S(2)}) async-start(bf16[1,16,24,256]{3,2,0,1:T(8,128)(2,1)} %add_convert_fusion), calls=%async_computation.4 | async-start | bytes 393216 | tf_op jit(solution)/shard_map/all_to_all | solution.py:118
  168.8 5.7 %all-to-all-done.4 = bf16[1,16,24,256]{3,2,0,1:T(8,128)(2,1)S(1)} async-done(((bf16[1,16,24,256]{3,2,0,1:T(8,128)(2,1)}), bf16[1,16,24,256]{3,2,0,1:T(8,128)(2,1)S(1)}, u32[]{:S(2)}, u32[]{:S(2)}) %all-to-all-start.4) | async-done | bytes 196640 | tf_op jit(solution)/shard_map/all_to_all | solution.py:118
  176.7 15.7 %all_to_all.36 = bf16[1,16,24,256]{3,2,0,1:T(8,128)(2,1)} all-to-all(bf16[1,16,24,256]{3,2,0,1:T(8,128)(2,1)S(1)} %fusion.94), channel_id=1, replica_groups=mesh['client'=16,'tensor'=8,'sdata'=2] {'client'}, dimensions={1} | all-to-all | bytes 393216 | tf_op jit(solution)/shard_map/all_to_all | solution.py:114
  192.5 23.7 %all-gather.5.cloned.1.call-done = bf16[1,384,2048]{2,1,0:T(8,128)(2,1)} async-done(((bf16[1,384,256]{2,1,0:T(8,128)(2,1)}), bf16[1,384,2048]{2,1,0:T(8,128)(2,1)}) %all-gather.5.cloned.1.call-update) | async-done | bytes 1572880 | tf_op jit(solution)/shard_map/all_gather | solution.py:140
  216.2 2.3 fusion.57
  218.5 1.7 fusion.21
  222.7 4.1 %convolution_convert_fusion.3 = bf16[2048,64]{0,1:T(8,128)(2,1)} fusion(bf16[64,4,384]{2,0,1:T(8,128)(2,1)S(1)} %bitcast.269, f32[4,384]{1,0:T(4,128)S(1)} %copy-done.27, f32[4,384]{1,0:T(4,128)S(1)} %get-tuple-element.27, f32[384,384,4]{1,0,2:T(8,128)} %copy-done.1, pred[384,384]{0,1:T(8,128)(4,1)S(1)} %copy-done.9, bf16[384,2048]{1,0:T(8,128)(2,1)} %param.12, ...), kind=kOutput, calls=%fused_computation.41 | convolution fusion | flops 182411264 | bytes 4560384 | tf_op jit(solution)/shard_map/transpose(jvp())/dot_general | solution.py:64
  226.9 3.4 %convolution_convert_fusion.2 = bf16[2048,256]{1,0:T(8,128)(2,1)} fusion(bf16[384,256]{0,1:T(8,128)(2,1)S(1)} %bitcast.267, bf16[384,2048]{1,0:T(8,128)(2,1)} %param.12, f32[2048]{0:T(1024)S(1)} %bitcast.277, f32[384]{0:T(512)S(1)} %copy-done.34), kind=kOutput, calls=%fused_computation.28 | convolution fusion | flops 405798912 | bytes 2827776 | tf_op jit(solution)/shard_map/transpose(jvp())/dot_general | solution.py:51
  232.5 2.2 convolution_convert_fusion.1
  236.0 72.6 %all_to_all.37 = bf16[32,64,640]{2,1,0:T(8,128)(2,1)S(1)} all-to-all(bf16[32,64,640]{2,1,0:T(8,128)(2,1)S(1)} %pad_maximum_fusion), channel_id=1, replica_groups=mesh['client'=16,'tensor'=8,'sdata'=2] {'client','sdata'}, dimensions={0} | all-to-all | bytes 5242880 | tf_op jit(solution)/shard_map/all_to_all | solution.py:18
  (136 shorter events, 30.6 us)
Async XLA Ops:
  7.2 118.2 %copy-start = (bf16[1,2048,512]{2,1,0:T(8,128)(2,1)S(1)}, bf16[1,2048,512]{2,1,0:T(8,128)(2,1)}, u32[]{:S(2)}) copy-start(bf16[1,2048,512]{2,1,0:T(8,128)(2,1)} %param.20) | copy-start | bytes 6291460
  7.3 12.5 %copy-start.8 = (pred[384,384]{0,1:T(8,128)(4,1)}, pred[384,384]{0,1:T(8,128)(4,1)S(1)}, u32[]{:S(2)}) copy-start(pred[384,384]{0,1:T(8,128)(4,1)S(1)} %iota_compare_fusion) | copy-start | bytes 442372
  8.1 8.2 %copy-start.31 = (f32[1,2048]{1,0:T(1,128)}, f32[1,2048]{1,0:T(1,128)S(1)}, u32[]{:S(2)}) copy-start(f32[1,2048]{1,0:T(1,128)S(1)} %mul.298) | copy-start | bytes 24580
  8.1 4.0 %copy-start.10 = (bf16[1,2048,256]{2,1,0:T(8,128)(2,1)S(1)}, bf16[1,2048,256]{2,1,0:T(8,128)(2,1)}, u32[]{:S(2)}) copy-start(bf16[1,2048,256]{2,1,0:T(8,128)(2,1)} %param.14) | copy-start | bytes 3145732
  10.0 6.2 %copy-start.33 = (f32[384]{0:T(512)}, f32[384]{0:T(512)S(1)}, u32[]{:S(2)}) copy-start(f32[384]{0:T(512)S(1)} %add_rsqrt_fusion.1) | copy-start | bytes 4612
  13.6 2.7 copy-start.6
  13.6 2.7 copy-start.36
  17.0 2.8 copy-start.38
  17.3 2.0 copy-start.22
  20.7 2.4 copy-start.16
  23.1 24.9 %all-to-all-start = ((bf16[8,384,256]{2,1,0:T(8,128)(2,1)}), bf16[8,384,256]{2,1,0:T(8,128)(2,1)}, u32[]{:S(2)}, u32[]{:S(2)}) async-start(bf16[8,384,256]{2,1,0:T(8,128)(2,1)} %bitcast.249), calls=%async_computation | async-start | bytes 3145728 | tf_op jit(solution)/shard_map/all_to_all | solution.py:18
  29.5 30.0 %copy-start.37 = (s32[16]{0:T(128)S(1)}, s32[16]{0:T(128)}, u32[]{:S(2)}) copy-start(s32[16]{0:T(128)} %param.23) | copy-start | bytes 196
  51.5 20.7 %all-to-all-start.1 = ((bf16[2,16,24,256]{3,2,0,1:T(8,128)(2,1)}), bf16[2,16,24,256]{3,2,0,1:T(8,128)(2,1)S(1)}, u32[]{:S(2)}, u32[]{:S(2)}) async-start(bf16[2,16,24,256]{3,2,0,1:T(8,128)(2,1)} %pad_maximum_fusion.1), calls=%async_computation.1 | async-start | bytes 786432 | tf_op jit(solution)/shard_map/all_to_all | solution.py:114
  59.5 57.4 %all-gather.3.cloned.1.call-start = ((), (), s32[]{:S(2)}) async-start(), calls=%async_computation.7 | async-start | bytes 3538944 | tf_op jit(solution)/shard_map/all_gather | solution.py:140
  119.3 4.2 %copy-start.29 = (f32[384]{0:T(512)}, f32[384]{0:T(512)S(1)}, u32[]{:S(2)}) copy-start(f32[384]{0:T(512)S(1)} %get-tuple-element.26) | copy-start | bytes 4612
  119.3 4.2 %copy-start.3 = (bf16[2,384,2048]{2,1,0:T(8,128)(2,1)S(1)}, bf16[2,384,2048]{2,1,0:T(8,128)(2,1)}, u32[]{:S(2)}) copy-start(bf16[2,384,2048]{2,1,0:T(8,128)(2,1)} %all-gather.3.cloned.1.call-done) | copy-start | bytes 9437188
  119.3 4.2 %copy-start.35 = (bf16[1,2048,512]{2,1,0:T(8,128)(2,1)S(1)}, bf16[1,2048,512]{2,1,0:T(8,128)(2,1)}, u32[]{:S(2)}) copy-start(bf16[1,2048,512]{2,1,0:T(8,128)(2,1)} %param.19) | copy-start | bytes 6291460
  131.6 4.2 %copy-start.4 = (bf16[2,384,2048]{2,1,0:T(8,128)(2,1)S(1)}, bf16[2,384,2048]{2,1,0:T(8,128)(2,1)}, u32[]{:S(2)}) copy-start(bf16[2,384,2048]{2,1,0:T(8,128)(2,1)} %all-gather.3.cloned.1.call-done) | copy-start | bytes 9437188
  131.6 4.2 %copy-start.28 = (f32[384]{0:T(512)S(1)}, f32[384]{0:T(512)}, u32[]{:S(2)}) copy-start(f32[384]{0:T(512)} %get-tuple-element.25) | copy-start | bytes 4612
  131.7 4.2 %copy-start.30 = (f32[384]{0:T(512)S(1)}, f32[384]{0:T(512)}, u32[]{:S(2)}) copy-start(f32[384]{0:T(512)} %copy-done.29) | copy-start | bytes 4612
  137.8 23.5 %all-to-all-start.3 = ((bf16[8,384,256]{2,1,0:T(8,128)(2,1)}), bf16[8,384,256]{2,1,0:T(8,128)(2,1)}, u32[]{:S(2)}, u32[]{:S(2)}) async-start(bf16[8,384,256]{2,1,0:T(8,128)(2,1)} %bitcast.250), calls=%async_computation.3 | async-start | bytes 3145728 | tf_op jit(solution)/shard_map/all_to_all | solution.py:18
  142.8 49.7 %copy-start.27 = (f32[4,384]{1,0:T(4,128)S(1)}, f32[4,384]{1,0:T(4,128)}, u32[]{:S(2)}) copy-start(f32[4,384]{1,0:T(4,128)} %copy-done.26) | copy-start | bytes 18436
  163.7 54.8 %copy-start.9 = (pred[384,384]{0,1:T(8,128)(4,1)S(1)}, pred[384,384]{0,1:T(8,128)(4,1)}, u32[]{:S(2)}) copy-start(pred[384,384]{0,1:T(8,128)(4,1)} %copy-done.8) | copy-start | bytes 442372
  163.7 10.7 %all-to-all-start.4 = ((bf16[1,16,24,256]{3,2,0,1:T(8,128)(2,1)}), bf16[1,16,24,256]{3,2,0,1:T(8,128)(2,1)S(1)}, u32[]{:S(2)}, u32[]{:S(2)}) async-start(bf16[1,16,24,256]{3,2,0,1:T(8,128)(2,1)} %add_convert_fusion), calls=%async_computation.4 | async-start | bytes 393216 | tf_op jit(solution)/shard_map/all_to_all | solution.py:118
  168.1 48.0 %all-gather.5.cloned.1.call-start = ((), (), s32[]{:S(2)}) async-start(), calls=%async_computation.8 | async-start | bytes 1769472 | tf_op jit(solution)/shard_map/all_gather | solution.py:140
  216.2 2.3 copy-start.2
  222.7 4.2 %copy-start.13 = (f32[384,64]{0,1:T(8,128)S(1)}, f32[384,64]{0,1:T(8,128)}, u32[]{:S(2)}) copy-start(f32[384,64]{0,1:T(8,128)} %copy-done.12) | copy-start | bytes 294916
  226.8 3.5 %copy-start.19 = (f32[384,32]{0,1:T(8,128)S(1)}, f32[384,32]{0,1:T(8,128)}, u32[]{:S(2)}) copy-start(f32[384,32]{0,1:T(8,128)} %copy-done.18) | copy-start | bytes 147460
  226.9 3.5 %copy-start.7 = (bf16[384,2048]{1,0:T(8,128)(2,1)S(1)}, bf16[384,2048]{1,0:T(8,128)(2,1)}, u32[]{:S(2)}) copy-start(bf16[384,2048]{1,0:T(8,128)(2,1)} %param.12) | copy-start | bytes 4718596
  226.9 3.5 %copy-start.23 = (f32[384,32]{0,1:T(8,128)S(1)}, f32[384,32]{0,1:T(8,128)}, u32[]{:S(2)}) copy-start(f32[384,32]{0,1:T(8,128)} %copy-done.22) | copy-start | bytes 147460
  230.3 2.2 copy-start.17
  232.5 2.3 copy-start.11
  (13 other events, 18.1 us)
Sparse Core Ops, SparseCore 0:
  86.9 29.9 all-gather.2
  192.6 23.5 all-gather.4
where the time goes:
time: 318 us; the launch traced here: 317 us
  waiting for transfers between devices  100 us (31%)
  blocking collectives  99.6 us (31%)
  matrix products  40.7 us (13%)
  starting transfers between devices  23.9 us (8%)
  other arithmetic  23.6 us (7%)
  between operations  14.7 us (5%)
  local copies, waits for them, and re-layouts  14.5 us (5%)
    all_to_all x1, blocking collectives, sum_at_owner(): lax.all_to_all(cut_along(value, dim, length), axis, 0, 0, tiled=True)  72.6 us
    all_gather x2, waiting for transfers between devices, widen_rows(): return lax.all_gather(stacked, 'tensor', axis=2, tiled=True)  53.1 us
    all_to_all x2, waiting for transfers between devices, sum_at_owner(): lax.all_to_all(cut_along(value, dim, length), axis, 0, 0, tiled=True)  31.3 us
    all_to_all x1, blocking collectives, over_clients(): lax.all_to_all(pieces, 'client', split_axis=1, concat_axis=1, tiled=True)  15.7 us
    all_to_all x2, starting transfers between devices, sum_at_owner(): lax.all_to_all(cut_along(value, dim, length), axis, 0, 0, tiled=True)  11.4 us
    all_to_all x1, blocking collectives, over_groups(): lax.all_to_all(pieces, 'sdata', split_axis=1, concat_axis=1, tiled=True)  11.3 us
    all_to_all x1, waiting for transfers between devices, over_clients(): lax.all_to_all(pieces, 'client', split_axis=1, concat_axis=1, tiled=True)  10.1 us
    all_to_all x1, starting transfers between devices, over_clients(): lax.all_to_all(pieces, 'client', split_axis=1, concat_axis=1, tiled=True)  8.01 us
  transfers between devices with their start and end apart: 6, of which 6 were waited for; matrix products, arithmetic and copies ran while one was open for 3% of the time, Pallas kernels for 0%

commit v1 on v0

--- a/solution.py
+++ b/solution.py
@@ -6,6 +6,13 @@
 from jax.sharding import PartitionSpec as P
 
 HEAD_DIM = 64
+
+
+def swapped_in(shard, name, d):
+    size = lax.axis_size(name)
+    blocks = jnp.stack([shard for _ in range(size)])
+    blocks = lax.all_to_all(blocks, name, split_axis=0, concat_axis=0)
+    return jnp.concatenate(blocks, axis=d)
 
 
 def cut_along(value, dim, length):
@@ -137,7 +144,7 @@
 
 
 def widen_rows(stacked):
-    return lax.all_gather(stacked, "tensor", axis=2, tiled=True)
+    return swapped_in(stacked, "tensor", 2)
 
 
 def local(

time: 318 us -> 330 us (1.038)
  starting transfers between devices: 23.9 us -> 38.7 us
  between operations: 14.7 us -> 1.26 us
  local copies, waits for them, and re-layouts: 14.5 us -> 24.6 us
  blocking collectives: 99.6 us -> 90.5 us
  waiting for transfers between devices: 100 us -> 106 us
    all_to_all x0 -> x2, waiting for transfers between devices: none -> 53.7 us  [swapped_in(): blocks = lax.all_to_all(blocks, name, split_axis=0, concat_axis=0)]
    all_gather x2 -> x0, waiting for transfers between devices: 53.1 us -> none  [widen_rows(): return lax.all_gather(stacked, 'tensor', axis=2, tiled=True)]
    all_to_all x0 -> x2, starting transfers between devices: none -> 14.2 us  [swapped_in(): blocks = lax.all_to_all(blocks, name, split_axis=0, concat_axis=0)]
    all_to_all x1, blocking collectives: 72.6 us -> 66.2 us  [sum_at_owner(): lax.all_to_all(cut_along(value, dim, length), axis, 0, 0, tiled=True)]
    all_to_all x0 -> x1, local copies, waits for them, and re-layouts: none -> 4.67 us  [swapped_in(): blocks = lax.all_to_all(blocks, name, split_axis=0, concat_axis=0)]
    slice x0 -> x1, other arithmetic: none -> 4.46 us  [local(): widened[1]]
    convert_element_type x0 -> x1, local copies, waits for them, and re-layouts: none -> 3.58 us  [server_pull(): rows_float = rows_in.astype(jnp.float32)]
    another operation x0 -> x3, local copies, waits for them, and re-layouts: none -> 3.47 us  [swapped_in(): blocks = jnp.stack([shard for _ in range(size)])]
  transfers between devices with their start and end apart: 6 -> 6, of which waited for: 6 -> 6; matrix products, arithmetic and copies ran while one was open for 3% -> 1% of each run, Pallas kernels for 0% -> 0%
where the time goes in v1:
time: 330 us; the launch traced here: 326 us
  waiting for transfers between devices  106 us (32%)
  blocking collectives  90.5 us (27%)
  matrix products  39.5 us (12%)
  starting transfers between devices  38.7 us (12%)
  other arithmetic  25.8 us (8%)
  local copies, waits for them, and re-layouts  24.6 us (7%)
    all_to_all x1, blocking collectives, sum_at_owner(): lax.all_to_all(cut_along(value, dim, length), axis, 0, 0, tiled=True)  66.2 us
    all_to_all x2, waiting for transfers between devices, swapped_in(): blocks = lax.all_to_all(blocks, name, split_axis=0, concat_axis=0)  53.7 us
    all_to_all x2, waiting for transfers between devices, sum_at_owner(): lax.all_to_all(cut_along(value, dim, length), axis, 0, 0, tiled=True)  34.7 us
    all_to_all x2, starting transfers between devices, swapped_in(): blocks = lax.all_to_all(blocks, name, split_axis=0, concat_axis=0)  14.2 us
    all_to_all x2, starting transfers between devices, sum_at_owner(): lax.all_to_all(cut_along(value, dim, length), axis, 0, 0, tiled=True)  13.1 us
    all_to_all x1, blocking collectives, over_clients(): lax.all_to_all(pieces, 'client', split_axis=1, concat_axis=1, tiled=True)  12.9 us
    all_to_all x1, waiting for transfers between devices, over_clients(): lax.all_to_all(pieces, 'client', split_axis=1, concat_axis=1, tiled=True)  11.4 us
    all_to_all x1, blocking collectives, over_groups(): lax.all_to_all(pieces, 'sdata', split_axis=1, concat_axis=1, tiled=True)  11.3 us
  transfers between devices with their start and end apart: 6, of which 6 were waited for; matrix products, arithmetic and copies ran while one was open for 1% of the time, Pallas kernels for 0%

profile of v1, /device:TPU:4, one launch (start us, length us, event | category | flops | bytes accessed | tf_op | source)
XLA Modules:
  0.0 326.4 jit_solution(9785524748324022834)
XLA Ops:
  0.7 1.9 fusion
  3.4 2.7 fusion.57
  9.6 2.5 fusion.22
  17.8 6.4 %all-to-all-start = ((bf16[8,384,256]{2,1,0:T(8,128)(2,1)}), bf16[8,384,256]{2,1,0:T(8,128)(2,1)}, u32[]{:S(2)}, u32[]{:S(2)}) async-start(bf16[8,384,256]{2,1,0:T(8,128)(2,1)} %bitcast.234), calls=%async_computation | async-start | bytes 3145728 | tf_op jit(solution)/shard_map/all_to_all | solution.py:25
  25.1 17.5 %all-to-all-done = bf16[8,384,256]{2,1,0:T(8,128)(2,1)} async-done(((bf16[8,384,256]{2,1,0:T(8,128)(2,1)}), bf16[8,384,256]{2,1,0:T(8,128)(2,1)}, u32[]{:S(2)}, u32[]{:S(2)}) %all-to-all-start) | async-done | bytes 1572896 | tf_op jit(solution)/shard_map/all_to_all | solution.py:25
  46.1 8.0 %all-to-all-start.1 = ((bf16[2,16,24,256]{3,2,0,1:T(8,128)(2,1)}), bf16[2,16,24,256]{3,2,0,1:T(8,128)(2,1)S(1)}, u32[]{:S(2)}, u32[]{:S(2)}) async-start(bf16[2,16,24,256]{3,2,0,1:T(8,128)(2,1)} %pad_maximum_fusion.1), calls=%async_computation.1 | async-start | bytes 786432 | tf_op jit(solution)/shard_map/all_to_all | solution.py:121
  55.4 11.4 %all-to-all-done.1 = bf16[2,16,24,256]{3,2,0,1:T(8,128)(2,1)S(1)} async-done(((bf16[2,16,24,256]{3,2,0,1:T(8,128)(2,1)}), bf16[2,16,24,256]{3,2,0,1:T(8,128)(2,1)S(1)}, u32[]{:S(2)}, u32[]{:S(2)}) %all-to-all-start.1) | async-done | bytes 393248 | tf_op jit(solution)/shard_map/all_to_all | solution.py:121
  67.5 11.3 %all_to_all.45 = bf16[2,16,24,256]{3,2,0,1:T(8,128)(2,1)S(1)} all-to-all(bf16[2,16,24,256]{3,2,0,1:T(8,128)(2,1)S(1)} %select_bitcast_fusion), channel_id=1, replica_groups=mesh['client'=16,'tensor'=8,'sdata'=2] {'sdata'}, dimensions={1} | all-to-all | bytes 786432 | tf_op jit(solution)/shard_map/all_to_all | solution.py:125
  78.9 2.0 stack.18
  80.9 7.3 %all-to-all-start.3 = ((bf16[8,2,384,256]{3,2,1,0:T(8,128)(2,1)}), bf16[8,2,384,256]{3,2,1,0:T(8,128)(2,1)}, u32[]{:S(2)}, u32[]{:S(2)}) async-start(bf16[8,2,384,256]{3,2,1,0:T(8,128)(2,1)} %stack.18), calls=%async_computation.3 | async-start | bytes 6291456 | tf_op jit(solution)/shard_map/all_to_all | solution.py:14
  88.2 35.3 %all-to-all-done.3 = bf16[8,2,384,256]{3,2,1,0:T(8,128)(2,1)} async-done(((bf16[8,2,384,256]{3,2,1,0:T(8,128)(2,1)}), bf16[8,2,384,256]{3,2,1,0:T(8,128)(2,1)}, u32[]{:S(2)}, u32[]{:S(2)}) %all-to-all-start.3) | async-done | bytes 3145760 | tf_op jit(solution)/shard_map/all_to_all | solution.py:14
  123.5 4.7 %copy.52 = bf16[8,2,384,256]{2,3,0,1:T(8,128)(2,1)} copy(bf16[8,2,384,256]{3,2,1,0:T(8,128)(2,1)} %all-to-all-done.3) | data formatting | bytes 6291456 | tf_op jit(solution)/shard_map/all_to_all | solution.py:14
  130.0 4.5 %fusion.100 = (bf16[1,384,8,256]{1,3,2,0:T(8,128)(2,1)}, f32[1,384,8,256]{1,3,2,0:T(8,128)}) fusion(bf16[2,384,8,256]{1,3,2,0:T(8,128)(2,1)} %bitcast.231), kind=kLoop, calls=%fused_computation.141 | loop fusion | flops 786432 | bytes 7864320 | tf_op jit(solution)/shard_map/slice | solution.py:183
  134.5 3.6 %copy.63 = f32[384,2048]{1,0:T(8,128)} copy(f32[384,2048]{0,1:T(8,128)} %bitcast.233) | data formatting | bytes 6291456 | tf_op jit(solution)/shard_map/convert_element_type | solution.py:94
  138.0 2.0 multiply_convert_fusion
  140.1 2.0 fusion.14
  143.0 2.0 fusion.19
  145.0 6.3 %fusion.12 = f32[384,2048]{1,0:T(8,128)} fusion(bf16[1,2048,512]{2,1,0:T(8,128)(2,1)} %param.19, f32[384,512]{1,0:T(8,128)} %fusion.19, bf16[384,2048]{0,1:T(8,128)(2,1)} %bitcast.244, bf16[1,2048,512]{2,1,0:T(8,128)(2,1)S(1)} %copy-done, f32[384,512]{1,0:T(8,128)} %fusion.14), kind=kOutput, calls=%fused_computation.35 | convolution fusion | flops 1612578816 | bytes 10485760 | tf_op jit(solution)/shard_map/dot_general | solution.py:108
  151.2 4.6 %multiply_reduce_fusion = (f32[384]{0:T(512)S(1)}, f32[384,2048]{1,0:T(8,128)S(1)}) fusion(f32[384,2048]{1,0:T(8,128)} %copy.63, f32[2048]{0:T(1024)S(1)} %bitcast.257, f32[384,2048]{1,0:T(8,128)} %fusion.12, bf16[1,2048,512]{2,1,0:T(8,128)(2,1)S(1)} %copy-done, f32[384,512]{1,0:T(8,128)} %fusion.19, f32[384,512]{1,0:T(8,128)} %fusion.14), kind=kOutput, calls=%fused_computation.10 | convolution fusion | flops 809631360 | bytes 13116928 | tf_op jit(solution)/shard_map/dot_general | solution.py:111
  157.7 6.7 %all-to-all-start.4 = ((bf16[8,384,256]{2,1,0:T(8,128)(2,1)}), bf16[8,384,256]{2,1,0:T(8,128)(2,1)S(1)}, u32[]{:S(2)}, u32[]{:S(2)}) async-start(bf16[8,384,256]{2,1,0:T(8,128)(2,1)} %bitcast.227), calls=%async_computation.4 | async-start | bytes 3145728 | tf_op jit(solution)/shard_map/all_to_all | solution.py:25
  165.7 17.1 %all-to-all-done.4 = bf16[8,384,256]{2,1,0:T(8,128)(2,1)S(1)} async-done(((bf16[8,384,256]{2,1,0:T(8,128)(2,1)}), bf16[8,384,256]{2,1,0:T(8,128)(2,1)S(1)}, u32[]{:S(2)}, u32[]{:S(2)}) %all-to-all-start.4) | async-done | bytes 1572896 | tf_op jit(solution)/shard_map/all_to_all | solution.py:25
  183.7 3.4 %all-to-all-start.5 = ((bf16[1,16,24,256]{3,2,0,1:T(8,128)(2,1)}), bf16[1,16,24,256]{3,2,0,1:T(8,128)(2,1)S(1)}, u32[]{:S(2)}, u32[]{:S(2)}) async-start(bf16[1,16,24,256]{3,2,0,1:T(8,128)(2,1)} %add_convert_fusion), calls=%async_computation.5 | async-start | bytes 393216 | tf_op jit(solution)/shard_map/all_to_all | solution.py:125
  187.2 6.3 %all-to-all-done.5 = bf16[1,16,24,256]{3,2,0,1:T(8,128)(2,1)S(1)} async-done(((bf16[1,16,24,256]{3,2,0,1:T(8,128)(2,1)}), bf16[1,16,24,256]{3,2,0,1:T(8,128)(2,1)S(1)}, u32[]{:S(2)}, u32[]{:S(2)}) %all-to-all-start.5) | async-done | bytes 196640 | tf_op jit(solution)/shard_map/all_to_all | solution.py:125
  194.1 12.9 %all_to_all.46 = bf16[1,16,24,256]{3,2,0,1:T(8,128)(2,1)S(1)} all-to-all(bf16[1,16,24,256]{3,2,0,1:T(8,128)(2,1)S(1)} %fusion.74), channel_id=1, replica_groups=mesh['client'=16,'tensor'=8,'sdata'=2] {'client'}, dimensions={1} | all-to-all | bytes 393216 | tf_op jit(solution)/shard_map/all_to_all | solution.py:121
  208.6 6.9 %all-to-all-start.7 = ((bf16[8,1,384,256]{2,3,1,0:T(8,128)(2,1)}), bf16[8,1,384,256]{2,3,1,0:T(8,128)(2,1)S(1)}, u32[]{:S(2)}, u32[]{:S(2)}) async-start(bf16[8,1,384,256]{2,3,1,0:T(8,128)(2,1)} %stack.19), calls=%async_computation.7 | async-start | bytes 3145728 | tf_op jit(solution)/shard_map/all_to_all | solution.py:14
  215.5 18.4 %all-to-all-done.7 = bf16[8,1,384,256]{2,3,1,0:T(8,128)(2,1)S(1)} async-done(((bf16[8,1,384,256]{2,3,1,0:T(8,128)(2,1)}), bf16[8,1,384,256]{2,3,1,0:T(8,128)(2,1)S(1)}, u32[]{:S(2)}, u32[]{:S(2)}) %all-to-all-start.7) | async-done | bytes 1572896 | tf_op jit(solution)/shard_map/all_to_all | solution.py:14
  235.4 4.1 %convolution_convert_fusion.3 = bf16[2048,64]{0,1:T(8,128)(2,1)} fusion(bf16[64,4,384]{2,0,1:T(8,128)(2,1)S(1)} %bitcast.264, f32[4,384]{1,0:T(4,128)S(1)} %fusion.93, f32[4,384]{1,0:T(4,128)S(1)} %get-tuple-element.29, f32[384,384,4]{1,0,2:T(8,128)} %copy-done.3, pred[384,384]{0,1:T(8,128)(4,1)S(1)} %iota_compare_fusion, bf16[384,2048]{1,0:T(8,128)(2,1)} %param.12, ...), kind=kOutput, calls=%fused_computation.33 | convolution fusion | flops 182411264 | bytes 4560384 | tf_op jit(solution)/shard_map/transpose(jvp())/dot_general | solution.py:71
  239.5 2.7 fusion.11
  244.1 2.0 broadcast_multiply_fusion
  250.1 2.2 convolution_convert_fusion.4
  254.9 2.3 convolution_convert_fusion.2
  258.4 66.2 %all_to_all.47 = bf16[32,64,640]{2,1,0:T(8,128)(2,1)S(1)} all-to-all(bf16[32,64,640]{2,1,0:T(8,128)(2,1)S(1)} %pad_maximum_fusion), channel_id=1, replica_groups=mesh['client'=16,'tensor'=8,'sdata'=2] {'client','sdata'}, dimensions={0} | all-to-all | bytes 5242880 | tf_op jit(solution)/shard_map/all_to_all | solution.py:25
  (137 shorter events, 37.9 us)
Async XLA Ops:
  0.6 144.3 %copy-start = (bf16[1,2048,512]{2,1,0:T(8,128)(2,1)S(1)}, bf16[1,2048,512]{2,1,0:T(8,128)(2,1)}, u32[]{:S(2)}) copy-start(bf16[1,2048,512]{2,1,0:T(8,128)(2,1)} %param.20) | copy-start | bytes 6291460
  0.7 5.4 %copy-start.5 = (bf16[384,2048]{1,0:T(8,128)(2,1)S(1)}, bf16[384,2048]{1,0:T(8,128)(2,1)}, u32[]{:S(2)}) copy-start(bf16[384,2048]{1,0:T(8,128)(2,1)} %param.12) | copy-start | bytes 4718596
  0.7 5.4 %copy-start.32 = (bf16[1,2048,64]{1,2,0:T(8,128)(2,1)S(1)}, bf16[1,2048,64]{1,2,0:T(8,128)(2,1)}, u32[]{:S(2)}) copy-start(bf16[1,2048,64]{1,2,0:T(8,128)(2,1)} %param.15) | copy-start | bytes 786436
  2.7 6.9 %copy-start.27 = (f32[384]{0:T(512)}, f32[384]{0:T(512)S(1)}, u32[]{:S(2)}) copy-start(f32[384]{0:T(512)S(1)} %add_rsqrt_fusion.1) | copy-start | bytes 4612
  3.4 6.1 %copy-start.24 = (f32[1,2048]{1,0:T(1,128)}, f32[1,2048]{1,0:T(1,128)S(1)}, u32[]{:S(2)}) copy-start(f32[1,2048]{1,0:T(1,128)S(1)} %mul.299) | copy-start | bytes 24580
  6.2 2.0 copy-start.9
  9.6 2.9 copy-start.17
  9.6 2.9 copy-start.19
  9.6 2.9 copy-start.20
  15.2 2.5 copy-start.14
  17.8 24.9 %all-to-all-start = ((bf16[8,384,256]{2,1,0:T(8,128)(2,1)}), bf16[8,384,256]{2,1,0:T(8,128)(2,1)}, u32[]{:S(2)}, u32[]{:S(2)}) async-start(bf16[8,384,256]{2,1,0:T(8,128)(2,1)} %bitcast.234), calls=%async_computation | async-start | bytes 3145728 | tf_op jit(solution)/shard_map/all_to_all | solution.py:25
  24.2 30.0 %copy-start.33 = (s32[16]{0:T(128)S(1)}, s32[16]{0:T(128)}, u32[]{:S(2)}) copy-start(s32[16]{0:T(128)} %param.23) | copy-start | bytes 196
  46.1 20.7 %all-to-all-start.1 = ((bf16[2,16,24,256]{3,2,0,1:T(8,128)(2,1)}), bf16[2,16,24,256]{3,2,0,1:T(8,128)(2,1)S(1)}, u32[]{:S(2)}, u32[]{:S(2)}) async-start(bf16[2,16,24,256]{3,2,0,1:T(8,128)(2,1)} %pad_maximum_fusion.1), calls=%async_computation.1 | async-start | bytes 786432 | tf_op jit(solution)/shard_map/all_to_all | solution.py:121
  80.9 7.3 %copy-start.23 = (bf16[1,2048]{1,0:T(2,128)(2,1)S(1)}, bf16[1,2048]{1,0:T(2,128)(2,1)}, u32[]{:S(2)}) copy-start(bf16[1,2048]{1,0:T(2,128)(2,1)} %param.18) | copy-start | bytes 12292
  80.9 42.6 %all-to-all-start.3 = ((bf16[8,2,384,256]{3,2,1,0:T(8,128)(2,1)}), bf16[8,2,384,256]{3,2,1,0:T(8,128)(2,1)}, u32[]{:S(2)}, u32[]{:S(2)}) async-start(bf16[8,2,384,256]{3,2,1,0:T(8,128)(2,1)} %stack.18), calls=%async_computation.3 | async-start | bytes 6291456 | tf_op jit(solution)/shard_map/all_to_all | solution.py:14
  138.0 2.1 copy-start.31
  140.0 2.0 copy-start.7
  140.1 2.0 copy-start.8
  140.1 2.8 copy-start.30
  151.2 4.6 %copy-start.2 = (f32[384,2048]{1,0:T(8,128)S(1)}, f32[384,2048]{1,0:T(8,128)}, u32[]{:S(2)}) copy-start(f32[384,2048]{1,0:T(8,128)} %copy.63) | copy-start | bytes 9437188
  157.7 25.1 %all-to-all-start.4 = ((bf16[8,384,256]{2,1,0:T(8,128)(2,1)}), bf16[8,384,256]{2,1,0:T(8,128)(2,1)S(1)}, u32[]{:S(2)}, u32[]{:S(2)}) async-start(bf16[8,384,256]{2,1,0:T(8,128)(2,1)} %bitcast.227), calls=%async_computation.4 | async-start | bytes 3145728 | tf_op jit(solution)/shard_map/all_to_all | solution.py:25
  183.7 9.8 %all-to-all-start.5 = ((bf16[1,16,24,256]{3,2,0,1:T(8,128)(2,1)}), bf16[1,16,24,256]{3,2,0,1:T(8,128)(2,1)S(1)}, u32[]{:S(2)}, u32[]{:S(2)}) async-start(bf16[1,16,24,256]{3,2,0,1:T(8,128)(2,1)} %add_convert_fusion), calls=%async_computation.5 | async-start | bytes 393216 | tf_op jit(solution)/shard_map/all_to_all | solution.py:125
  207.2 26.6 %copy-start.11 = (bf16[1,2048,256]{2,1,0:T(8,128)(2,1)S(1)}, bf16[1,2048,256]{2,1,0:T(8,128)(2,1)}, u32[]{:S(2)}) copy-start(bf16[1,2048,256]{2,1,0:T(8,128)(2,1)} %param.17) | copy-start | bytes 3145732
  208.6 25.3 %all-to-all-start.7 = ((bf16[8,1,384,256]{2,3,1,0:T(8,128)(2,1)}), bf16[8,1,384,256]{2,3,1,0:T(8,128)(2,1)S(1)}, u32[]{:S(2)}, u32[]{:S(2)}) async-start(bf16[8,1,384,256]{2,3,1,0:T(8,128)(2,1)} %stack.19), calls=%async_computation.7 | async-start | bytes 3145728 | tf_op jit(solution)/shard_map/all_to_all | solution.py:14
  215.5 19.2 %copy-start.15 = (bf16[64,4,384]{2,0,1:T(8,128)(2,1)S(1)}, bf16[64,4,384]{2,0,1:T(8,128)(2,1)}, u32[]{:S(2)}) copy-start(bf16[64,4,384]{2,0,1:T(8,128)(2,1)} %copy-done.14) | copy-start | bytes 589828
  235.4 4.1 %copy-start.35 = (bf16[384,64,1]{0,1,2:T(8,128)(2,1)S(1)}, bf16[384,64,1]{0,1,2:T(8,128)(2,1)}, u32[]{:S(2)}) copy-start(bf16[384,64,1]{0,1,2:T(8,128)(2,1)} %fusion.57) | copy-start | bytes 147460
  239.5 2.7 copy-start.4
  239.5 2.7 copy-start.13
  244.1 6.0 %copy-start.6 = (bf16[384,2048]{1,0:T(8,128)(2,1)S(1)}, bf16[384,2048]{1,0:T(8,128)(2,1)}, u32[]{:S(2)}) copy-start(bf16[384,2048]{1,0:T(8,128)(2,1)} %param.12) | copy-start | bytes 4718596
  250.1 4.8 %copy-start.26 = (f32[1,2048]{1,0:T(1,128)S(1)}, f32[1,2048]{1,0:T(1,128)}, u32[]{:S(2)}) copy-start(f32[1,2048]{1,0:T(1,128)} %copy-done.24) | copy-start | bytes 24580
  250.1 4.8 %copy-start.29 = (f32[384]{0:T(512)S(1)}, f32[384]{0:T(512)}, u32[]{:S(2)}) copy-start(f32[384]{0:T(512)} %copy-done.27) | copy-start | bytes 4612
  258.4 67.9 %copy-start.1 = (bf16[1,2048,512]{2,1,0:T(8,128)(2,1)S(1)}, bf16[1,2048,512]{2,1,0:T(8,128)(2,1)}, u32[]{:S(2)}) copy-start(bf16[1,2048,512]{2,1,0:T(8,128)(2,1)} %param.20) | copy-start | bytes 6291460
  (10 other events, 11.5 us)
